TPU v7x, 256 devices: a whole 4x4x8 slice. The times are simulated.
256 devices in a mesh: expert: 64 (over x, z, core), tensor: 4 (over y).
Axes of the slice: x: 4, y: 4, z: 8, core: 2. Of those that a mesh axis runs over, the one named last changes fastest.
Arguments:
- tokens: bfloat16 [8192, 3584], P('expert', 'tensor'), may hold values from -6 to 6
- expert_ids: int32 [8192, 4], P('expert'), may hold values from 0 to 63, all different within a row; in each aligned block of 128 rows (0 to 127, 128 to 255, ...) at most 12 rows name the same one
- gate_values: bfloat16 [8192, 4], P('expert'), may hold values from 0.049804688 to 0.3984375
- w_gate: bfloat16 [64, 3584, 1024], P('expert', None, 'tensor'), may hold values from -0.09375 to 0.09375
- w_up: bfloat16 [64, 3584, 1024], P('expert', None, 'tensor'), may hold values from -0.09375 to 0.09375
- w_down: bfloat16 [64, 1024, 3584], P('expert', 'tensor'), may hold values from -0.1875 to 0.1875
- shared_gate: bfloat16 [3584, 1024], P(None, 'tensor'), may hold values from -0.09375 to 0.09375
- shared_up: bfloat16 [3584, 1024], P(None, 'tensor'), may hold values from -0.09375 to 0.09375
- shared_down: bfloat16 [1024, 3584], P('tensor'), may hold values from -0.1875 to 0.1875
Outputs:
- moe_output: bfloat16 [8192, 3584], P('expert', 'tensor')
Inputs may be any that keep to these rules, and one draw needn't show every extreme that they name: `expert_ids`: each token names 4 different experts. Among the 128 tokens of one index of the expert axis (aligned blocks of 128 rows) no expert is named by more than 12 tokens, a bound that some block reaches.
All inputs are finite; a program needn't handle non-finite values.
Results may differ from a plain program's by a relative error of at most 0.013.
Values may be sent and summed in bfloat16 or wider, within the bound.
No kernel may reach another device: no remote copies, remote signals or barrier semaphores. Data moves between devices by JAX's collectives and lax.ppermute only.
A program may use at most 64 MiB of HBM per device.

v0:
```python
import jax
import jax.numpy as jnp
from jax import lax
from jax.sharding import Mesh
from jax.sharding import PartitionSpec as P

EXPERT = ("expert_0", "expert_1", "expert_2")


def in_order(tiles, dim):
    shape = list(tiles.shape[1:])
    shape[dim] *= tiles.shape[0]
    return jnp.moveaxis(tiles, 0, dim).reshape(shape)


def from_everyone(x, axis):
    copies = jnp.broadcast_to(x, (lax.axis_size(axis), *x.shape))
    return lax.all_to_all(copies, axis, split_axis=0, concat_axis=0, tiled=True)


def collect(x, axis, dim):
    return in_order(from_everyone(x, axis), dim)


def in_blocks(x, dim, devices):
    before, after = (x.shape[:dim], x.shape[dim + 1 :])
    return jnp.moveaxis(x.reshape(*before, devices, -1, *after), dim, 0)


def sent_and_summed(x, axis, dim):
    tiles = in_blocks(x, dim, lax.axis_size(axis))
    arrived = lax.all_to_all(tiles, axis, split_axis=0, concat_axis=0, tiled=True)
    return arrived.astype(jnp.float32).sum(axis=0)


def turned_blocks(tiles, axes, sequence):
    shape = [lax.axis_size(a) for a in axes]
    tiles = tiles.reshape(*shape, *tiles.shape[1:])
    for k in sequence:
        tiles = lax.all_to_all(tiles, axes[k], split_axis=k, concat_axis=k, tiled=True)
    return tiles.reshape(-1, *tiles.shape[len(axes) :])


def core_and_chips(x, groups, sequence, split_dim, concat_dim):
    devices = lax.axis_size(groups[0]) * lax.axis_size(groups[1])
    tiles = in_blocks(x, split_dim, devices)
    return in_order(turned_blocks(tiles, groups, sequence), concat_dim)


def per_device(
    tokens, expert_ids, gate_values, w_gate, w_up, w_down, shared_gate, shared_up, shared_down
):
    tok_dev, narrow = tokens.shape
    top_count = expert_ids.shape[1]
    per_lane, features, quarter = w_gate.shape
    lane_count = lax.axis_size(EXPERT)
    experts_all = lane_count * per_lane
    capacity = min(tok_dev, 3 * tok_dev * top_count // (2 * experts_all))
    total_rows = experts_all * capacity
    numbers = jnp.arange(experts_all, dtype=jnp.int32)
    onehot = (expert_ids[:, :, None] == numbers).astype(jnp.int32)
    per_token = jnp.sum(onehot, axis=1)
    earlier = jnp.cumsum(per_token, axis=0) - per_token
    slot_index = jnp.sum(onehot * earlier[:, None, :], axis=2)
    target = expert_ids * capacity + slot_index
    token_index = jnp.repeat(jnp.arange(tok_dev, dtype=jnp.int32), top_count)
    owners = jnp.full((total_rows,), tok_dev, jnp.int32).at[target.reshape(-1)].set(token_index)
    features_all = collect(tokens, "tensor", 1)
    shared_gate_sums = jnp.dot(features_all, shared_gate, preferred_element_type=jnp.float32)
    shared_up_sums = jnp.dot(features_all, shared_up, preferred_element_type=jnp.float32)
    shared_hidden = (jax.nn.silu(shared_gate_sums) * shared_up_sums).astype(jnp.bfloat16)
    shared_partial = jnp.dot(shared_hidden, shared_down, preferred_element_type=jnp.float32)
    padded = jnp.concatenate([tokens, jnp.zeros((1, narrow), jnp.bfloat16)], axis=0)
    outgoing = padded[owners].reshape(lane_count, per_lane * capacity, narrow)
    arrived = lax.all_to_all(outgoing, EXPERT, split_axis=0, concat_axis=0, tiled=True)
    arrived = arrived.reshape(lane_count, per_lane, capacity, narrow)
    block_rows = lax.all_gather(arrived, "tensor", axis=3, tiled=True)
    gate_more = jnp.einsum("sjcd,jdf->sjcf", block_rows, w_gate, preferred_element_type=jnp.float32)
    up_more = jnp.einsum("sjcd,jdf->sjcf", block_rows, w_up, preferred_element_type=jnp.float32)
    hidden = (jax.nn.silu(gate_more) * up_more).astype(jnp.bfloat16)
    partial_value = jnp.einsum("sjcf,jfd->sjcd", hidden, w_down, preferred_element_type=jnp.float32)
    summed = sent_and_summed(partial_value.astype(jnp.bfloat16), "tensor", 3)
    returned = core_and_chips(
        summed.reshape(lane_count, per_lane * capacity, narrow).astype(jnp.bfloat16),
        (("expert_0", "expert_1"), "expert_2"),
        (1, 0),
        0,
        0,
    ).astype(jnp.float32)
    picked = returned.reshape(total_rows, narrow)[target]
    routed = jnp.sum(gate_values.astype(jnp.float32)[:, :, None] * picked, axis=1)
    shared_total = sent_and_summed(shared_partial.astype(jnp.bfloat16), "tensor", 1)
    return (routed + shared_total).astype(jnp.bfloat16)


def solution(mesh):
    torus = Mesh(
        mesh.devices.reshape(4, 8, 2, mesh.shape["tensor"]),
        ("expert_0", "expert_1", "expert_2", "tensor"),
    )
    placed = (
        P(EXPERT, "tensor"),
        P(EXPERT, None),
        P(EXPERT, None),
        P(EXPERT, None, "tensor"),
        P(EXPERT, None, "tensor"),
        P(EXPERT, "tensor", None),
        P(None, "tensor"),
        P(None, "tensor"),
        P("tensor", None),
    )
    return jax.shard_map(
        per_device, mesh=torus, in_specs=placed, out_specs=P(EXPERT, "tensor"), check_vma=False
    )
```

profile of v0, /device:TPU:32, one launch (start us, length us, event | category | flops | bytes accessed | tf_op | source)
XLA Modules:
  0.0 321.1 jit_solution(12613605834629810689)
XLA Ops:
  6.5 0.8 convert_reduce_fusion.1
  7.7 0.7 select_reduce_fusion
  8.5 0.7 compare_select_fusion.2
  9.5 2.4 scatter_custom_fusion
  12.0 1.0 concatenate.3
  12.9 2.8 gather_fusion
  15.8 1.4 reshape.100
  17.2 56.0 %all_to_all.30 = bf16[64,12,896]{2,1,0:T(8,128)(2,1)S(1)} all-to-all(bf16[64,12,896]{2,1,0:T(8,128)(2,1)} %reshape.100), channel_id=1, replica_groups=mesh['expert_0'=4,'expert_1'=8,'expert_2'=2,'tensor'=4] {'expert_0','exp..., dimensions={0} | all-to-all | bytes 2752512 | tf_op jit(solution)/shard_map/all_to_all | solution.py:75
  73.2 1.4 copy.49
  74.9 1.1 broadcast_in_dim.25
  75.9 4.5 %all-to-all-start.4 = ((bf16[4,128,896]{1,2,0:T(8,128)(2,1)}), bf16[4,128,896]{1,2,0:T(8,128)(2,1)S(1)}, u32[]{:S(2)}, u32[]{:S(2)}) async-start(bf16[4,128,896]{1,2,0:T(8,128)(2,1)} %broadcast_in_dim.25), calls=%async_computation.4 | async-start | bytes 1835008 | tf_op jit(solution)/shard_map/all_to_all | solution.py:18
  80.4 58.3 %all-gather.3.cloned.1.call-done = bf16[64,12,3584]{2,0,1:T(8,128)(2,1)} async-done(((bf16[64,12,896]{2,0,1:T(8,128)(2,1)}), bf16[64,12,3584]{2,0,1:T(8,128)(2,1)}) %all-gather.3.cloned.1.call-update) | async-done | bytes 5505040 | tf_op jit(solution)/shard_map/all_gather | solution.py:77
  138.6 5.6 %fusion.5 = f32[64,1,12,256]{3,0,2,1:T(8,128)} fusion(bf16[64,12,3584]{2,0,1:T(8,128)(2,1)} %all-gather.3.cloned.1.call-done, bf16[1,3584,256]{2,1,0:T(8,128)(2,1)} %param.12), kind=kOutput, calls=%fused_computation.14 | convolution fusion | flops 1409286144 | bytes 8126464 | tf_op jit(solution)/shard_map/sjcd,jdf->sjcf/dot_general | solution.py:78
  144.3 11.5 %convolution_convert_fusion = bf16[64,12,3584]{2,0,1:T(8,128)(2,1)} fusion(bf16[1,256,3584]{2,1,0:T(8,128)(2,1)S(1)} %copy-done, bf16[64,12,3584]{2,0,1:T(8,128)(2,1)} %all-gather.3.cloned.1.call-done, bf16[1,3584,256]{2,1,0:T(8,128)(2,1)} %param.13, f32[64,1,12,256]{3,0,2,1:T(8,128)} %fusion.5), kind=kOutput, calls=%fused_computation.3 | convolution fusion | flops 2822504448 | bytes 15466496 | tf_op jit(solution)/shard_map/sjcf,jfd->sjcd/dot_general | solution.py:81
  155.7 5.8 %copy.65 = bf16[1,12,8,4,8,896]{5,4,2,1,0,3:T(8,128)(2,1)} copy(bf16[1,12,8,4,8,896]{5,4,3,2,1,0:T(8,128)(2,1)} %bitcast.85) | data formatting | bytes 11010048 | tf_op jit(solution)/shard_map/reshape | solution.py:27
  161.6 5.4 %all-to-all-start.1 = ((bf16[4,64,1,12,896]{4,1,3,2,0:T(8,128)(2,1)}), bf16[4,64,1,12,896]{4,1,3,2,0:T(8,128)(2,1)}, u32[]{:S(2)}, u32[]{:S(2)}) async-start(bf16[4,64,1,12,896]{4,1,3,2,0:T(8,128)(2,1)} %bitcast.82), calls=%async_computation.1 | async-start | bytes 11010048 | tf_op jit(solution)/shard_map/all_to_all | solution.py:32
  167.5 3.3 %convolution_convert_fusion.1 = bf16[128,3584]{1,0:T(8,128)(2,1)S(1)} fusion(bf16[256,3584]{1,0:T(8,128)(2,1)} %param.17, bf16[128,3584]{0,1:T(8,128)(2,1)S(1)} %bitcast.84, bf16[3584,256]{1,0:T(8,128)(2,1)} %param.16, f32[128,256]{1,0:T(8,128)S(1)} %fusion.39), kind=kOutput, calls=%fused_computation.5 | convolution fusion | flops 470417408 | bytes 5636096 | tf_op jit(solution)/shard_map/dot_general | solution.py:72
  170.8 1.0 copy.66
  171.8 58.3 %all-to-all-done.1 = bf16[4,64,1,12,896]{4,1,3,2,0:T(8,128)(2,1)} async-done(((bf16[4,64,1,12,896]{4,1,3,2,0:T(8,128)(2,1)}), bf16[4,64,1,12,896]{4,1,3,2,0:T(8,128)(2,1)}, u32[]{:S(2)}, u32[]{:S(2)}) %all-to-all-start.1) | async-done | bytes 5505056 | tf_op jit(solution)/shard_map/all_to_all | solution.py:32
  230.1 3.6 %reduce_sum.50 = bf16[64,12,896]{2,0,1:T(8,128)(2,1)S(1)} reduce(bf16[4,64,1,12,896]{4,1,3,2,0:T(8,128)(2,1)} %all-to-all-done.1, bf16[]{:T(256)} %constant.8.clone.1), dimensions={0,2}, to_apply=%region_4.5 | reduce | flops 2064384 | bytes 6881282 | tf_op jit(solution)/shard_map/reduce_sum | solution.py:33
  234.5 4.8 %all_to_all.31 = bf16[32,2,1,12,896]{4,0,3,2,1:T(8,128)(2,1)S(1)} all-to-all(bf16[32,2,1,12,896]{4,0,3,2,1:T(8,128)(2,1)S(1)} %copy.52), channel_id=1, replica_groups=mesh['expert_0'=4,'expert_1'=8,'expert_2'=2,'tensor'=4] {'expert_2'}, dimensions={1} | all-to-all | bytes 2752512 | tf_op jit(solution)/shard_map/all_to_all | solution.py:40
  239.3 3.5 %all-to-all-start.5 = ((bf16[4,128,896]{2,1,0:T(8,128)(2,1)}), bf16[4,128,896]{2,1,0:T(8,128)(2,1)S(1)}, u32[]{:S(2)}, u32[]{:S(2)}) async-start(bf16[4,128,896]{2,1,0:T(8,128)(2,1)} %bitcast.81), calls=%async_computation.5 | async-start | bytes 1835008 | tf_op jit(solution)/shard_map/all_to_all | solution.py:32
  242.8 2.5 copy.53
  245.3 11.7 %all-to-all-done.5 = bf16[4,128,896]{2,1,0:T(8,128)(2,1)S(1)} async-done(((bf16[4,128,896]{2,1,0:T(8,128)(2,1)}), bf16[4,128,896]{2,1,0:T(8,128)(2,1)S(1)}, u32[]{:S(2)}, u32[]{:S(2)}) %all-to-all-start.5) | async-done | bytes 917536 | tf_op jit(solution)/shard_map/all_to_all | solution.py:32
  257.1 6.9 %all-to-all-start.3 = ((bf16[32,2,1,12,896]{4,1,3,2,0:T(2,128)(2,1)}), bf16[32,2,1,12,896]{4,1,3,2,0:T(2,128)(2,1)S(1)}, u32[]{:S(2)}, u32[]{:S(2)}) async-start(bf16[32,2,1,12,896]{4,1,3,2,0:T(2,128)(2,1)} %copy.53), calls=%async_computation.3 | async-start | bytes 2752512 | tf_op jit(solution)/shard_map/all_to_all | solution.py:40
  264.4 34.2 %all-to-all-done.3 = bf16[32,2,1,12,896]{4,1,3,2,0:T(2,128)(2,1)S(1)} async-done(((bf16[32,2,1,12,896]{4,1,3,2,0:T(2,128)(2,1)}), bf16[32,2,1,12,896]{4,1,3,2,0:T(2,128)(2,1)S(1)}, u32[]{:S(2)}, u32[]{:S(2)}) %all-to-all-start.3) | async-done | bytes 1376288 | tf_op jit(solution)/shard_map/all_to_all | solution.py:40
  299.0 3.4 %copy.55 = f32[32,2,1,12,896]{4,3,1,0,2:T(8,128)} copy(f32[32,2,1,12,896]{4,0,3,2,1:T(8,128)S(1)} %copy_convert_fusion) | data formatting | bytes 5505024 | tf_op jit(solution)/shard_map/convert_element_type | solution.py:89
  302.4 2.9 reshape.110
  305.3 2.7 gather_fusion.1
  307.9 2.9 reshape.120
  310.9 2.7 multiply_reduce_fusion
  313.6 0.7 add_convert_fusion
  (34 shorter events, 2.9 us)
Async XLA Ops:
  6.5 137.7 %copy-start = (bf16[1,256,3584]{2,1,0:T(8,128)(2,1)S(1)}, bf16[1,256,3584]{2,1,0:T(8,128)(2,1)}, u32[]{:S(2)}) copy-start(bf16[1,256,3584]{2,1,0:T(8,128)(2,1)} %param.14) | copy-start | bytes 5505028
  6.5 132.1 %all-gather.3.cloned.1.call-start = ((), (), s32[]{:S(2)}) async-start(), calls=%async_computation.6 | async-start | bytes 6881280 | tf_op jit(solution)/shard_map/all_gather | solution.py:77
  73.2 1.4 copy-start.3
  75.9 85.7 %all-to-all-start.4 = ((bf16[4,128,896]{1,2,0:T(8,128)(2,1)}), bf16[4,128,896]{1,2,0:T(8,128)(2,1)S(1)}, u32[]{:S(2)}, u32[]{:S(2)}) async-start(bf16[4,128,896]{1,2,0:T(8,128)(2,1)} %broadcast_in_dim.25), calls=%async_computation.4 | async-start | bytes 1835008 | tf_op jit(solution)/shard_map/all_to_all | solution.py:18
  161.6 5.5 %copy-start.2 = (bf16[3584,256]{1,0:T(8,128)(2,1)S(1)}, bf16[3584,256]{1,0:T(8,128)(2,1)}, u32[]{:S(2)}) copy-start(bf16[3584,256]{1,0:T(8,128)(2,1)} %param.15) | copy-start | bytes 5505028
  161.6 68.5 %all-to-all-start.1 = ((bf16[4,64,1,12,896]{4,1,3,2,0:T(8,128)(2,1)}), bf16[4,64,1,12,896]{4,1,3,2,0:T(8,128)(2,1)}, u32[]{:S(2)}, u32[]{:S(2)}) async-start(bf16[4,64,1,12,896]{4,1,3,2,0:T(8,128)(2,1)} %bitcast.82), calls=%async_computation.1 | async-start | bytes 11010048 | tf_op jit(solution)/shard_map/all_to_all | solution.py:32
  239.3 17.7 %all-to-all-start.5 = ((bf16[4,128,896]{2,1,0:T(8,128)(2,1)}), bf16[4,128,896]{2,1,0:T(8,128)(2,1)S(1)}, u32[]{:S(2)}, u32[]{:S(2)}) async-start(bf16[4,128,896]{2,1,0:T(8,128)(2,1)} %bitcast.81), calls=%async_computation.5 | async-start | bytes 1835008 | tf_op jit(solution)/shard_map/all_to_all | solution.py:32
  245.3 18.8 %copy-start.4 = (bf16[128,4]{0,1:T(4,128)(2,1)S(1)}, bf16[128,4]{0,1:T(4,128)(2,1)}, u32[]{:S(2)}) copy-start(bf16[128,4]{0,1:T(4,128)(2,1)} %param.11) | copy-start | bytes 3076
  257.1 41.6 %all-to-all-start.3 = ((bf16[32,2,1,12,896]{4,1,3,2,0:T(2,128)(2,1)}), bf16[32,2,1,12,896]{4,1,3,2,0:T(2,128)(2,1)S(1)}, u32[]{:S(2)}, u32[]{:S(2)}) async-start(bf16[32,2,1,12,896]{4,1,3,2,0:T(2,128)(2,1)} %copy.53), calls=%async_computation.3 | async-start | bytes 2752512 | tf_op jit(solution)/shard_map/all_to_all | solution.py:40
  307.9 6.4 %copy-start.1 = (bf16[1,256,3584]{2,1,0:T(8,128)(2,1)S(1)}, bf16[1,256,3584]{2,1,0:T(8,128)(2,1)}, u32[]{:S(2)}) copy-start(bf16[1,256,3584]{2,1,0:T(8,128)(2,1)} %param.14) | copy-start | bytes 5505028
Sparse Core Ops, SparseCore 0:
  74.8 63.8 all-gather.2
where the time goes:
time: 322 us; the launch traced here: 321 us
  waiting for transfers between devices  163 us (51%)
  blocking collectives  60.9 us (19%)
  local copies, waits for them, and re-layouts  33.1 us (10%)
  matrix products  20.8 us (6%)
  starting transfers between devices  20.3 us (6%)
  between operations  13.6 us (4%)
  other arithmetic  9.92 us (3%)
    all_to_all x2, waiting for transfers between devices, sent_and_summed(): lax.all_to_all(tiles, axis, split_axis=0, concat_axis=0, tiled=True)  70.1 us
    all_gather x1, waiting for transfers between devices, per_device(): block_rows = lax.all_gather(arrived, 'tensor', axis=3, tiled=True)  58.3 us
    all_to_all x1, blocking collectives, per_device(): lax.all_to_all(outgoing, EXPERT, split_axis=0, concat_axis=0, tiled=True)  56 us
    all_to_all x1, waiting for transfers between devices, turned_blocks(): lax.all_to_all(tiles, axes[k], split_axis=k, concat_axis=k, tiled=True)  34.2 us
    dot_general x1, matrix products, per_device(): jnp.einsum('sjcf,jfd->sjcd', hidden, w_down, preferred_element_type=jnp.f...  11.5 us
    all_to_all x2, starting transfers between devices, sent_and_summed(): lax.all_to_all(tiles, axis, split_axis=0, concat_axis=0, tiled=True)  8.94 us
    all_to_all x1, starting transfers between devices, turned_blocks(): lax.all_to_all(tiles, axes[k], split_axis=k, concat_axis=k, tiled=True)  6.87 us
    reshape x2, local copies, waits for them, and re-layouts, in_blocks(): return jnp.moveaxis(x.reshape(*before, devices, -1, *after), dim, 0)  6.86 us
  transfers between devices with their start and end apart: 5, of which 4 were waited for; matrix products, arithmetic and copies ran while one was open for 10% of the time, Pallas kernels for 0%

commit v1 on v0

--- a/solution.py
+++ b/solution.py
@@ -74,7 +74,9 @@
     outgoing = padded[owners].reshape(lane_count, per_lane * capacity, narrow)
     arrived = lax.all_to_all(outgoing, EXPERT, split_axis=0, concat_axis=0, tiled=True)
     arrived = arrived.reshape(lane_count, per_lane, capacity, narrow)
-    block_rows = lax.all_gather(arrived, "tensor", axis=3, tiled=True)
+    block_rows = jnp.concatenate(
+        lax.all_to_all(jnp.stack([arrived] * lax.axis_size("tensor")), "tensor", 0, 0), axis=3
+    )
     gate_more = jnp.einsum("sjcd,jdf->sjcf", block_rows, w_gate, preferred_element_type=jnp.float32)
     up_more = jnp.einsum("sjcd,jdf->sjcf", block_rows, w_up, preferred_element_type=jnp.float32)
     hidden = (jax.nn.silu(gate_more) * up_more).astype(jnp.bfloat16)

time: 322 us -> 339 us (1.053)
  local copies, waits for them, and re-layouts: 33.1 us -> 54 us
  between operations: 13.6 us -> 0.23 us
  starting transfers between devices: 20.3 us -> 25 us
  waiting for transfers between devices: 163 us -> 167 us
    all_to_all x0 -> x1, waiting for transfers between devices: none -> 63.3 us  [per_device(): lax.all_to_all(jnp.stack([arrived] * lax.axis_size('tensor')), 'tensor',...]
    all_gather x1 -> x0, waiting for transfers between devices: 58.3 us -> none  [per_device(): block_rows = lax.all_gather(arrived, 'tensor', axis=3, tiled=True)]
    another operation x0 -> x2, local copies, waits for them, and re-layouts: none -> 12.7 us
    reshape x0 -> x1, local copies, waits for them, and re-layouts: none -> 9.27 us  [per_device(): jnp.concatenate(lax.all_to_all(jnp.stack([arrived] * lax.axis_size('tenso...]
    all_to_all x0 -> x1, starting transfers between devices: none -> 5.22 us  [per_device(): lax.all_to_all(jnp.stack([arrived] * lax.axis_size('tensor')), 'tensor',...]
  transfers between devices with their start and end apart: 5 -> 5, of which waited for: 4 -> 4; matrix products, arithmetic and copies ran while one was open for 10% -> 15% of each run, Pallas kernels for 0% -> 0%
where the time goes in v1:
time: 339 us; the launch traced here: 338 us
  waiting for transfers between devices  167 us (49%)
  blocking collectives  60.9 us (18%)
  local copies, waits for them, and re-layouts  54 us (16%)
  starting transfers between devices  25 us (7%)
  matrix products  20.8 us (6%)
  other arithmetic  9.92 us (3%)
    all_to_all x2, waiting for transfers between devices, sent_and_summed(): lax.all_to_all(tiles, axis, split_axis=0, concat_axis=0, tiled=True)  69.4 us
    all_to_all x1, waiting for transfers between devices, per_device(): lax.all_to_all(jnp.stack([arrived] * lax.axis_size('tensor')), 'tensor',...  63.3 us
    all_to_all x1, blocking collectives, per_device(): lax.all_to_all(outgoing, EXPERT, split_axis=0, concat_axis=0, tiled=True)  56 us
    all_to_all x1, waiting for transfers between devices, turned_blocks(): lax.all_to_all(tiles, axes[k], split_axis=k, concat_axis=k, tiled=True)  34.2 us
    dot_general x1, matrix products, per_device(): jnp.einsum('sjcf,jfd->sjcd', hidden, w_down, preferred_element_type=jnp.f...  11.5 us
    another operation x1, local copies, waits for them, and re-layouts  9.47 us
    reshape x1, local copies, waits for them, and re-layouts, per_device(): jnp.concatenate(lax.all_to_all(jnp.stack([arrived] * lax.axis_size('tenso...  9.27 us
    all_to_all x2, starting transfers between devices, sent_and_summed(): lax.all_to_all(tiles, axis, split_axis=0, concat_axis=0, tiled=True)  8.98 us
  transfers between devices with their start and end apart: 5, of which 4 were waited for; matrix products, arithmetic and copies ran while one was open for 15% of the time, Pallas kernels for 0%

profile of v1, /device:TPU:32, one launch (start us, length us, event | category | flops | bytes accessed | tf_op | source)
XLA Modules:
  0.0 337.8 jit_solution(10408534605004385266)
XLA Ops:
  0.0 0.8 convert_reduce_fusion.1
  3.0 2.4 scatter_custom_fusion
  5.4 1.0 concatenate.3
  6.4 2.8 gather_fusion
  9.2 1.4 reshape.105
  10.7 56.0 %all_to_all.35 = bf16[64,12,896]{2,1,0:T(8,128)(2,1)S(1)} all-to-all(bf16[64,12,896]{2,1,0:T(8,128)(2,1)} %reshape.105), channel_id=1, replica_groups=mesh['expert_0'=4,'expert_1'=8,'expert_2'=2,'tensor'=4] {'expert_0','exp..., dimensions={0} | all-to-all | bytes 2752512 | tf_op jit(solution)/shard_map/all_to_all | solution.py:75
  67.0 3.2 stack.3
  70.2 5.2 %all-to-all-start.1 = ((bf16[4,64,1,12,896]{4,1,3,2,0:T(8,128)(2,1)}), bf16[4,64,1,12,896]{4,1,3,2,0:T(8,128)(2,1)}, u32[]{:S(2)}, u32[]{:S(2)}) async-start(bf16[4,64,1,12,896]{4,1,3,2,0:T(8,128)(2,1)} %stack.3), calls=%async_computation.1 | async-start | bytes 11010048 | tf_op jit(solution)/shard_map/all_to_all | solution.py:78
  75.7 63.3 %all-to-all-done.1 = bf16[4,64,1,12,896]{4,1,3,2,0:T(8,128)(2,1)} async-done(((bf16[4,64,1,12,896]{4,1,3,2,0:T(8,128)(2,1)}), bf16[4,64,1,12,896]{4,1,3,2,0:T(8,128)(2,1)}, u32[]{:S(2)}, u32[]{:S(2)}) %all-to-all-start.1) | async-done | bytes 5505056 | tf_op jit(solution)/shard_map/all_to_all | solution.py:78
  138.9 1.1 broadcast_in_dim.25
  140.0 3.7 %all-to-all-start.5 = ((bf16[4,128,896]{1,2,0:T(8,128)(2,1)}), bf16[4,128,896]{1,2,0:T(8,128)(2,1)S(1)}, u32[]{:S(2)}, u32[]{:S(2)}) async-start(bf16[4,128,896]{1,2,0:T(8,128)(2,1)} %broadcast_in_dim.25), calls=%async_computation.5 | async-start | bytes 1835008 | tf_op jit(solution)/shard_map/all_to_all | solution.py:18
  143.7 9.3 %copy.53 = bf16[64,1,12,4,896]{4,3,0,2,1:T(4,128)(2,1)} copy(bf16[64,1,12,4,896]{4,0,2,1,3:T(8,128)(2,1)} %bitcast.1) | data formatting | bytes 11010048 | tf_op jit(solution)/shard_map/reshape | solution.py:77
  152.9 9.5 %reshape.107 = bf16[64,12,3584]{2,0,1:T(8,128)(2,1)} reshape(bf16[64,1,12,4,896]{4,3,0,2,1:T(4,128)(2,1)} %copy.53) | data formatting | bytes 11010048 | tf_op jit(solution)/shard_map/reshape.2
  162.4 5.6 %fusion.5 = f32[64,1,12,256]{3,0,2,1:T(8,128)} fusion(bf16[64,12,3584]{2,0,1:T(8,128)(2,1)} %reshape.107, bf16[1,3584,256]{2,1,0:T(8,128)(2,1)} %param.12), kind=kOutput, calls=%fused_computation.14 | convolution fusion | flops 1409286144 | bytes 8126464 | tf_op jit(solution)/shard_map/sjcd,jdf->sjcf/dot_general | solution.py:80
  168.0 11.5 %convolution_convert_fusion = bf16[64,12,3584]{2,0,1:T(8,128)(2,1)} fusion(bf16[1,256,3584]{2,1,0:T(8,128)(2,1)S(1)} %copy-done, bf16[64,12,3584]{2,0,1:T(8,128)(2,1)} %reshape.107, bf16[1,3584,256]{2,1,0:T(8,128)(2,1)} %param.13, f32[64,1,12,256]{3,0,2,1:T(8,128)} %fusion.5), kind=kOutput, calls=%fused_computation.3 | convolution fusion | flops 2822504448 | bytes 15466496 | tf_op jit(solution)/shard_map/sjcf,jfd->sjcd/dot_general | solution.py:83
  179.5 5.8 %copy.69 = bf16[1,12,8,4,8,896]{5,4,2,1,0,3:T(8,128)(2,1)} copy(bf16[1,12,8,4,8,896]{5,4,3,2,1,0:T(8,128)(2,1)} %bitcast.88) | data formatting | bytes 11010048 | tf_op jit(solution)/shard_map/reshape | solution.py:27
  185.4 5.5 %all-to-all-start.2 = ((bf16[4,64,1,12,896]{4,1,3,2,0:T(8,128)(2,1)}), bf16[4,64,1,12,896]{4,1,3,2,0:T(8,128)(2,1)}, u32[]{:S(2)}, u32[]{:S(2)}) async-start(bf16[4,64,1,12,896]{4,1,3,2,0:T(8,128)(2,1)} %bitcast.85), calls=%async_computation.2 | async-start | bytes 11010048 | tf_op jit(solution)/shard_map/all_to_all | solution.py:32
  191.3 3.3 convolution_convert_fusion.1
  194.6 1.0 copy.70
  195.6 57.7 %all-to-all-done.2 = bf16[4,64,1,12,896]{4,1,3,2,0:T(8,128)(2,1)} async-done(((bf16[4,64,1,12,896]{4,1,3,2,0:T(8,128)(2,1)}), bf16[4,64,1,12,896]{4,1,3,2,0:T(8,128)(2,1)}, u32[]{:S(2)}, u32[]{:S(2)}) %all-to-all-start.2) | async-done | bytes 5505056 | tf_op jit(solution)/shard_map/all_to_all | solution.py:32
  253.3 3.6 %reduce_sum.50 = bf16[64,12,896]{2,0,1:T(8,128)(2,1)S(1)} reduce(bf16[4,64,1,12,896]{4,1,3,2,0:T(8,128)(2,1)} %all-to-all-done.2, bf16[]{:T(256)} %constant.8.clone.1), dimensions={0,2}, to_apply=%region_4.5 | reduce | flops 2064384 | bytes 6881282 | tf_op jit(solution)/shard_map/reduce_sum | solution.py:33
  257.6 4.8 %all_to_all.36 = bf16[32,2,1,12,896]{4,0,3,2,1:T(8,128)(2,1)S(1)} all-to-all(bf16[32,2,1,12,896]{4,0,3,2,1:T(8,128)(2,1)S(1)} %copy.56), channel_id=1, replica_groups=mesh['expert_0'=4,'expert_1'=8,'expert_2'=2,'tensor'=4] {'expert_2'}, dimensions={1} | all-to-all | bytes 2752512 | tf_op jit(solution)/shard_map/all_to_all | solution.py:40
  262.5 3.5 %all-to-all-start.6 = ((bf16[4,128,896]{2,1,0:T(8,128)(2,1)}), bf16[4,128,896]{2,1,0:T(8,128)(2,1)S(1)}, u32[]{:S(2)}, u32[]{:S(2)}) async-start(bf16[4,128,896]{2,1,0:T(8,128)(2,1)} %bitcast.84), calls=%async_computation.6 | async-start | bytes 1835008 | tf_op jit(solution)/shard_map/all_to_all | solution.py:32
  266.0 2.5 copy.57
  268.5 11.7 %all-to-all-done.6 = bf16[4,128,896]{2,1,0:T(8,128)(2,1)S(1)} async-done(((bf16[4,128,896]{2,1,0:T(8,128)(2,1)}), bf16[4,128,896]{2,1,0:T(8,128)(2,1)S(1)}, u32[]{:S(2)}, u32[]{:S(2)}) %all-to-all-start.6) | async-done | bytes 917536 | tf_op jit(solution)/shard_map/all_to_all | solution.py:32
  280.2 7.2 %all-to-all-start.4 = ((bf16[32,2,1,12,896]{4,1,3,2,0:T(2,128)(2,1)}), bf16[32,2,1,12,896]{4,1,3,2,0:T(2,128)(2,1)S(1)}, u32[]{:S(2)}, u32[]{:S(2)}) async-start(bf16[32,2,1,12,896]{4,1,3,2,0:T(2,128)(2,1)} %copy.57), calls=%async_computation.4 | async-start | bytes 2752512 | tf_op jit(solution)/shard_map/all_to_all | solution.py:40
  287.9 34.2 %all-to-all-done.4 = bf16[32,2,1,12,896]{4,1,3,2,0:T(2,128)(2,1)S(1)} async-done(((bf16[32,2,1,12,896]{4,1,3,2,0:T(2,128)(2,1)}), bf16[32,2,1,12,896]{4,1,3,2,0:T(2,128)(2,1)S(1)}, u32[]{:S(2)}, u32[]{:S(2)}) %all-to-all-start.4) | async-done | bytes 1376288 | tf_op jit(solution)/shard_map/all_to_all | solution.py:40
  322.4 3.4 %copy.59 = f32[32,2,1,12,896]{4,3,1,0,2:T(8,128)} copy(f32[32,2,1,12,896]{4,0,3,2,1:T(8,128)S(1)} %copy_convert_fusion) | data formatting | bytes 5505024 | tf_op jit(solution)/shard_map/convert_element_type | solution.py:91
  325.9 2.9 reshape.115
  328.7 2.7 gather_fusion.1
  331.4 2.9 reshape.125
  334.3 2.7 multiply_reduce_fusion
  (36 shorter events, 5.3 us)
Async XLA Ops:
  0.0 168.0 %copy-start = (bf16[1,256,3584]{2,1,0:T(8,128)(2,1)S(1)}, bf16[1,256,3584]{2,1,0:T(8,128)(2,1)}, u32[]{:S(2)}) copy-start(bf16[1,256,3584]{2,1,0:T(8,128)(2,1)} %param.14) | copy-start | bytes 5505028
  70.2 5.2 %copy-start.3 = (bf16[128,896]{1,0:T(8,128)(2,1)S(1)}, bf16[128,896]{1,0:T(8,128)(2,1)}, u32[]{:S(2)}) copy-start(bf16[128,896]{1,0:T(8,128)(2,1)} %param.9) | copy-start | bytes 688132
  70.2 68.7 %all-to-all-start.1 = ((bf16[4,64,1,12,896]{4,1,3,2,0:T(8,128)(2,1)}), bf16[4,64,1,12,896]{4,1,3,2,0:T(8,128)(2,1)}, u32[]{:S(2)}, u32[]{:S(2)}) async-start(bf16[4,64,1,12,896]{4,1,3,2,0:T(8,128)(2,1)} %stack.3), calls=%async_computation.1 | async-start | bytes 11010048 | tf_op jit(solution)/shard_map/all_to_all | solution.py:78
  140.0 45.4 %all-to-all-start.5 = ((bf16[4,128,896]{1,2,0:T(8,128)(2,1)}), bf16[4,128,896]{1,2,0:T(8,128)(2,1)S(1)}, u32[]{:S(2)}, u32[]{:S(2)}) async-start(bf16[4,128,896]{1,2,0:T(8,128)(2,1)} %broadcast_in_dim.25), calls=%async_computation.5 | async-start | bytes 1835008 | tf_op jit(solution)/shard_map/all_to_all | solution.py:18
  185.4 5.5 %copy-start.2 = (bf16[3584,256]{1,0:T(8,128)(2,1)S(1)}, bf16[3584,256]{1,0:T(8,128)(2,1)}, u32[]{:S(2)}) copy-start(bf16[3584,256]{1,0:T(8,128)(2,1)} %param.15) | copy-start | bytes 5505028
  185.4 67.9 %all-to-all-start.2 = ((bf16[4,64,1,12,896]{4,1,3,2,0:T(8,128)(2,1)}), bf16[4,64,1,12,896]{4,1,3,2,0:T(8,128)(2,1)}, u32[]{:S(2)}, u32[]{:S(2)}) async-start(bf16[4,64,1,12,896]{4,1,3,2,0:T(8,128)(2,1)} %bitcast.85), calls=%async_computation.2 | async-start | bytes 11010048 | tf_op jit(solution)/shard_map/all_to_all | solution.py:32
  262.5 17.7 %all-to-all-start.6 = ((bf16[4,128,896]{2,1,0:T(8,128)(2,1)}), bf16[4,128,896]{2,1,0:T(8,128)(2,1)S(1)}, u32[]{:S(2)}, u32[]{:S(2)}) async-start(bf16[4,128,896]{2,1,0:T(8,128)(2,1)} %bitcast.84), calls=%async_computation.6 | async-start | bytes 1835008 | tf_op jit(solution)/shard_map/all_to_all | solution.py:32
  268.5 19.1 %copy-start.4 = (bf16[128,4]{0,1:T(4,128)(2,1)S(1)}, bf16[128,4]{0,1:T(4,128)(2,1)}, u32[]{:S(2)}) copy-start(bf16[128,4]{0,1:T(4,128)(2,1)} %param.11) | copy-start | bytes 3076
  280.2 41.9 %all-to-all-start.4 = ((bf16[32,2,1,12,896]{4,1,3,2,0:T(2,128)(2,1)}), bf16[32,2,1,12,896]{4,1,3,2,0:T(2,128)(2,1)S(1)}, u32[]{:S(2)}, u32[]{:S(2)}) async-start(bf16[32,2,1,12,896]{4,1,3,2,0:T(2,128)(2,1)} %copy.57), calls=%async_computation.4 | async-start | bytes 2752512 | tf_op jit(solution)/shard_map/all_to_all | solution.py:40
  331.4 6.4 %copy-start.1 = (bf16[1,256,3584]{2,1,0:T(8,128)(2,1)S(1)}, bf16[1,256,3584]{2,1,0:T(8,128)(2,1)}, u32[]{:S(2)}) copy-start(bf16[1,256,3584]{2,1,0:T(8,128)(2,1)} %param.14) | copy-start | bytes 5505028
